TPU v7x, 32 devices: a whole 2x2x4 slice. The times are simulated.
32 devices in a mesh: grp: 2 (over y), row: 4 (over z), head: 2 (over x), br: 2 (over core).
Axes of the slice: x: 2, y: 2, z: 4, core: 2. Of those that a mesh axis runs over, the one named last changes fastest.
Arguments:
- pair_acts: float32 [16, 8, 128], P(('grp', 'row', 'head')), parts along dimension 0, may hold values from -6 to 6
- alignment: float32 [64, 8, 256], P(('grp', 'br'), ('row', 'head')), parts along dimension 0, may hold values from -6 to 6
- align_mask: int32 [64, 8], P('grp', ('row', 'head')), parts along dimension 0, may hold values from 0 to 1
- residue_mask: int32 [16], P('grp'), parts along dimension 0, may hold values from 0 to 1, as said below
- align_gain: float32 [256], replicated, may hold values from 0.25 to 1.75
- outer_in: float32 [256, 64], replicated, may hold values from -0.375 to 0.375
- outer_out: float32 [1024, 128], replicated, may hold values from -1 to 1
- tri_gain: float32 [2, 128], replicated, may hold values from 0.25 to 1.75
- tri_in: float32 [2, 128, 4, 128], P(None, None, 'br'), may hold values from -5 to 5
- tri_bias: float32 [2, 128, 4], P(None, None, 'br'), may hold values from -0.5 to 0.5
- tri_out: float32 [2, 4, 32, 128], P(None, 'br'), may hold values from -0.5 to 0.5
- pair_cotangent: float32 [16, 8, 128], P(('grp', 'row', 'head')), parts along dimension 0, may hold values from -6 to 6
Outputs:
- pair_out: float32 [16, 8, 128], P(('grp', 'row', 'head')), parts along dimension 0
- pair_grad: float32 [16, 8, 128], P(('grp', 'row', 'head')), parts along dimension 0
There are 2 independent parts, one for each index of `grp`. A program takes and returns all parts, laid end to end along the dimension named above; an argument that names none is the same for every part. Nothing has to cross between parts.
Inputs may be any that keep to these rules, and one draw needn't show every extreme that they name: `residue_mask`: 1 at residue 0, and 0 at one or more residues; `align_mask`: 1 at every residue of sequence 0 of each part.
All inputs are finite; a program needn't handle non-finite values.
Results may differ from a plain program's by a relative error of at most 0.0003.
Values sent between devices are 32-bit elements; how exact they have to be, the bound alone decides.
No kernel may reach another device: no remote copies, remote signals or barrier semaphores. Data moves between devices by JAX's collectives and lax.ppermute only.
A program may use at most 64 MiB of HBM per device.

v0:
```python
import jax
import jax.numpy as jnp
from jax import lax
from jax.sharding import PartitionSpec as P

OPC = 32
PRECISE = lax.Precision.HIGHEST
EPSILON = 1e-05
MASK_SHIFT = 1000000000.0


def normalize(values, scales):
    average = jnp.mean(values, axis=-1, keepdims=True)
    centred = values - average
    spread = jnp.mean(centred * centred, axis=-1, keepdims=True)
    return centred * lax.rsqrt(spread + EPSILON) * scales


def core_total(values):
    return lax.psum(values, "br")


def reorient(values):
    turned = jnp.swapaxes(values, 0, 1)
    return lax.all_to_all(turned, ("row", "head"), split_axis=0, concat_axis=1, tiled=True)


def prepare(values, scales, weight_in, weight_bias):
    normed = normalize(values, scales)
    projected = jnp.einsum("ijc,chd->ijhd", normed, weight_in, precision=PRECISE)
    bias_local = jnp.einsum("jkc,ch->hjk", normed, weight_bias, precision=PRECISE)
    return (projected, bias_local)


def attend(projected, bias_full, key_shift, weight_out):
    head_size = projected.shape[-1] // 4
    queries = projected[..., :head_size]
    key_proj = projected[..., head_size : 2 * head_size]
    value_proj = projected[..., 2 * head_size : 3 * head_size]
    gating = projected[..., 3 * head_size :]
    logits = jnp.einsum("ijhd,ikhd->ihjk", queries, key_proj, precision=PRECISE) * head_size ** (
        -0.5
    )
    logits = logits + bias_full[None] + key_shift
    attention = jax.nn.softmax(logits, axis=-1)
    attended = jnp.einsum("ihjk,ikhd->ijhd", attention, value_proj, precision=PRECISE)
    gated_out = jax.nn.sigmoid(gating) * attended
    return jnp.einsum("ijhd,hdc->ijc", gated_out, weight_out, precision=PRECISE)


def tri_forward(rows_in, scales, weight_in, weight_bias, weight_out, key_shift, pair_mask):

    def local_prep(values):
        return prepare(values, scales, weight_in, weight_bias)

    (projected, bias_local), pull_prep = jax.vjp(local_prep, rows_in)
    bias_full = lax.all_gather(bias_local, ("row", "head"), axis=1, tiled=True)

    def local_attend(proj_in, bias_in):
        return attend(proj_in, bias_in, key_shift, weight_out)

    partial_out, pull_attend = jax.vjp(local_attend, projected, bias_full)
    total_out = core_total(partial_out)
    return (rows_in + total_out * pair_mask, (pull_prep, pull_attend))


def tri_backward(grad_out, saved, pair_mask):
    pull_prep, pull_attend = saved
    grad_proj, grad_bias = pull_attend(grad_out * pair_mask)
    grad_local = lax.psum_scatter(grad_bias, ("row", "head"), scatter_dimension=1, tiled=True)
    (grad_rows,) = pull_prep((grad_proj, grad_local))
    return grad_out + core_total(grad_rows)


def body(
    pair_acts,
    alignment,
    align_mask,
    residue_mask,
    align_gain,
    outer_in,
    outer_out,
    tri_gain,
    tri_in,
    tri_bias,
    tri_out,
    pair_cotangent,
):
    row_count = pair_acts.shape[0]
    live = residue_mask.astype(jnp.float32)
    key_shift = (live - 1.0) * MASK_SHIFT
    row_live = lax.dynamic_slice_in_dim(
        live, lax.axis_index(("row", "head")) * row_count, row_count, 0
    )
    pair_mask = row_live[:, None, None] * live[None, :, None]
    seq_count = alignment.shape[0]
    mask_all = align_mask.astype(jnp.float32)
    mask_own = lax.dynamic_slice_in_dim(mask_all, lax.axis_index("br") * seq_count, seq_count, 0)
    normed = normalize(alignment, align_gain)
    projected = jnp.einsum("snc,ck->snk", normed, outer_in, precision=PRECISE)
    left_part = projected[..., :OPC] * mask_own[..., None]
    right_part = jnp.swapaxes(projected[..., OPC:] * mask_own[..., None], 1, 2)
    right_all, mask_cols = (
        lax.all_gather(right_part, ("row", "head"), axis=2, tiled=True),
        lax.all_gather(mask_all, ("row", "head"), axis=1, tiled=True),
    )
    counts = jnp.einsum("si,sj->ij", mask_all, mask_cols, precision=PRECISE)
    table = outer_out.reshape(OPC, OPC, outer_out.shape[-1])
    mixed_left = jnp.einsum("sip,pqc->siqc", left_part, table, precision=PRECISE)
    partial_outer = jnp.einsum("siqc,sqj->ijc", mixed_left, right_all, precision=PRECISE)
    outer_sum = core_total(partial_outer)
    pair_one = pair_acts + outer_sum / counts[..., None]
    pair_two, saved_start = tri_forward(
        pair_one, tri_gain[0], tri_in[0], tri_bias[0], tri_out[0], key_shift, pair_mask
    )
    turned_two = reorient(pair_two)
    turned_three, saved_end = tri_forward(
        turned_two, tri_gain[1], tri_in[1], tri_bias[1], tri_out[1], key_shift, pair_mask
    )
    pair_out = reorient(turned_three)
    grad_turned = reorient(pair_cotangent)
    grad_turned = tri_backward(grad_turned, saved_end, pair_mask)
    grad_two = reorient(grad_turned)
    pair_grad = tri_backward(grad_two, saved_start, pair_mask)
    return (pair_out, pair_grad)


def solution(mesh):
    in_specs = (
        P(("grp", "row", "head"), None, None),
        P(("grp", "br"), ("row", "head"), None),
        P("grp", ("row", "head")),
        P("grp"),
        P(),
        P(),
        P(),
        P(),
        P(None, None, "br", None),
        P(None, None, "br"),
        P(None, "br", None, None),
        P(("grp", "row", "head"), None, None),
    )
    out_specs = (P(("grp", "row", "head"), None, None), P(("grp", "row", "head"), None, None))
    return jax.shard_map(body, mesh=mesh, in_specs=in_specs, out_specs=out_specs, check_vma=False)
```

profile of v0, /device:TPU:0, one launch (start us, length us, event | category | flops | bytes accessed | tf_op | source)
XLA Modules:
  0.0 188.4 jit_solution(10134027815885279675)
XLA Ops:
  0.7 1.0 reduce_sum.121
  2.0 0.7 convert_bitcast_fusion
  2.6 0.8 multiply_multiply_fusion
  3.7 32.3 %all_gather.12 = f32[16,32,8]{1,0,2:T(8,128)S(1)} all-gather(f32[16,32,1]{1,0,2:T(8,128)S(1)} %fusion.30), channel_id=1, replica_groups=mesh['grp'=2,'row'=4,'head'=2,'br'=2] {'row','head'}, dimensions={2}, use_global_device_ids=true | all-gather | bytes 18432 | tf_op jit(solution)/shard_map/all_gather | solution.py:104
  36.9 0.7 convolution_bitcast_fusion.17
  37.6 2.5 %psum.35 = f32[1,8,128]{2,1,0:T(8,128)S(1)} all-reduce(f32[1,8,128]{2,1,0:T(8,128)S(1)} %convolution_bitcast_fusion.17), channel_id=1, replica_groups=mesh['grp'=2,'row'=4,'head'=2,'br'=2] {'br'}, use_global_device_ids=true, to_apply=%region_2.0 | all-reduce | flops 1024 | bytes 8192 | tf_op jit(solution)/shard_map/psum | solution.py:20
  40.0 20.4 %all-gather.2 = f32[8,1,32]{2,1,0:T(1,128)S(1)} all-gather(f32[1,1,32]{2,1,0:T(1,128)S(1)} %get-tuple-element.16), channel_id=1, replica_groups=mesh['grp'=2,'row'=4,'head'=2,'br'=2] {'row','head'}, dimensions={0}, use_global_device_ids=true | all-gather | bytes 1152 | tf_op jit(solution)/shard_map/all_gather | solution.py:105
  65.1 16.3 %all-gather.3 = f32[8,8,2]{1,2,0:T(2,128)S(1)} all-gather(f32[1,8,2]{1,2,0:T(2,128)S(1)} %convolution_bitcast_fusion.19), channel_id=2, replica_groups=mesh['grp'=2,'row'=4,'head'=2,'br'=2] {'row','head'}, dimensions={0}, use_global_device_ids=true | all-gather | bytes 576 | tf_op jit(solution)/shard_map/all_gather | solution.py:57
  82.8 2.5 %psum.36 = f32[1,8,128]{2,1,0:T(8,128)S(1)} all-reduce(f32[1,8,128]{2,1,0:T(8,128)S(1)} %convolution_bitcast_fusion.16), channel_id=1, replica_groups=mesh['grp'=2,'row'=4,'head'=2,'br'=2] {'br'}, use_global_device_ids=true, to_apply=%region_7.0 | all-reduce | flops 1024 | bytes 8192 | tf_op jit(solution)/shard_map/psum | solution.py:20
  85.2 0.7 multiply_add_fusion
  85.9 3.3 %all-to-all-start = ((f32[8,1,128]{2,1,0:T(1,128)}), f32[8,1,128]{2,1,0:T(1,128)S(1)}, u32[]{:S(2)}, u32[]{:S(2)}) async-start(f32[8,1,128]{2,1,0:T(1,128)} %bitcast.32), calls=%async_computation | async-start | bytes 8192 | tf_op jit(solution)/shard_map/all_to_all | solution.py:25
  90.5 5.1 %all-to-all-done = f32[8,1,128]{2,1,0:T(1,128)S(1)} async-done(((f32[8,1,128]{2,1,0:T(1,128)}), f32[8,1,128]{2,1,0:T(1,128)S(1)}, u32[]{:S(2)}, u32[]{:S(2)}) %all-to-all-start) | async-done | bytes 4128 | tf_op jit(solution)/shard_map/all_to_all | solution.py:25
  95.6 3.3 %all-to-all-start.2 = ((f32[8,1,128]{2,1,0:T(1,128)}), f32[8,1,128]{2,1,0:T(1,128)S(1)}, u32[]{:S(2)}, u32[]{:S(2)}) async-start(f32[8,1,128]{2,1,0:T(1,128)} %bitcast.54), calls=%async_computation.2 | async-start | bytes 8192 | tf_op jit(solution)/shard_map/all_to_all | solution.py:25
  99.5 20.9 %all-gather.4 = f32[8,8,2]{1,2,0:T(2,128)S(1)} all-gather(f32[1,8,2]{1,2,0:T(2,128)S(1)} %convolution_bitcast_fusion.18), channel_id=3, replica_groups=mesh['grp'=2,'row'=4,'head'=2,'br'=2] {'row','head'}, dimensions={0}, use_global_device_ids=true | all-gather | bytes 576 | tf_op jit(solution)/shard_map/all_gather | solution.py:57
  122.7 17.4 %all-reduce.8 = f32[2,8,8]{2,0,1:T(2,128)S(1)} all-reduce(f32[2,8,8]{2,0,1:T(2,128)S(1)} %copy.49), channel_id=4, replica_groups=mesh['grp'=2,'row'=4,'head'=2,'br'=2] {'row','head'}, use_global_device_ids=true, to_apply=%region_14.0.clone | all-reduce | flops 128 | bytes 1024
  140.0 0.8 fusion.92
  141.6 2.5 %psum.38 = f32[1,8,128]{2,1,0:T(8,128)S(1)} all-reduce(f32[1,8,128]{2,1,0:T(8,128)S(1)} %add_bitcast_fusion), channel_id=1, replica_groups=mesh['grp'=2,'row'=4,'head'=2,'br'=2] {'br'}, use_global_device_ids=true, to_apply=%region_17.0 | all-reduce | flops 1024 | bytes 8192 | tf_op jit(solution)/shard_map/psum | solution.py:20
  144.6 3.3 %all-to-all-start.3 = ((f32[8,1,128]{2,1,0:T(1,128)}), f32[8,1,128]{2,1,0:T(1,128)S(1)}, u32[]{:S(2)}, u32[]{:S(2)}) async-start(f32[8,1,128]{2,1,0:T(1,128)} %bitcast.75), calls=%async_computation.3 | async-start | bytes 8192 | tf_op jit(solution)/shard_map/all_to_all | solution.py:25
  148.2 6.1 %all-to-all-done.3 = f32[8,1,128]{2,1,0:T(1,128)S(1)} async-done(((f32[8,1,128]{2,1,0:T(1,128)}), f32[8,1,128]{2,1,0:T(1,128)S(1)}, u32[]{:S(2)}, u32[]{:S(2)}) %all-to-all-start.3) | async-done | bytes 4128 | tf_op jit(solution)/shard_map/all_to_all | solution.py:25
  155.6 17.9 %all-reduce.9 = f32[2,8,8]{2,0,1:T(2,128)S(1)} all-reduce(f32[2,8,8]{2,0,1:T(2,128)S(1)} %copy.52), channel_id=5, replica_groups=mesh['grp'=2,'row'=4,'head'=2,'br'=2] {'row','head'}, use_global_device_ids=true, to_apply=%region_19.0.clone | all-reduce | flops 128 | bytes 1024
  173.5 0.8 fusion.91
  175.1 2.5 %all-reduce.10 = (f32[1,8,128]{2,1,0:T(8,128)S(1)}, f32[1,8,128]{2,1,0:T(8,128)S(1)}) all-reduce(f32[1,8,128]{2,1,0:T(8,128)S(1)} %convolution_bitcast_fusion.15, f32[1,8,128]{2,1,0:T(8,128)S(1)} %broadcast_add_fusion), channel_id=1, replica_groups=mesh['grp'=2,'row'=4,'head'=2,'br'=2] {'br'}, use_global_device_ids=true, to_apply=%region_12.0 | all-reduce | flops 2048 | bytes 16384 | tf_op jit(solution)/shard_map/psum | solution.py:20
  178.2 3.3 %all-to-all-start.1 = ((f32[8,1,128]{2,1,0:T(1,128)}), f32[8,1,128]{2,1,0:T(1,128)S(1)}, u32[]{:S(2)}, u32[]{:S(2)}) async-start(f32[8,1,128]{2,1,0:T(1,128)} %bitcast.52), calls=%async_computation.1 | async-start | bytes 8192 | tf_op jit(solution)/shard_map/all_to_all | solution.py:25
  182.1 5.8 %all-to-all-done.1 = f32[8,1,128]{2,1,0:T(1,128)S(1)} async-done(((f32[8,1,128]{2,1,0:T(1,128)}), f32[8,1,128]{2,1,0:T(1,128)S(1)}, u32[]{:S(2)}, u32[]{:S(2)}) %all-to-all-start.1) | async-done | bytes 4128 | tf_op jit(solution)/shard_map/all_to_all | solution.py:25
  (101 shorter events, 16.6 us)
Async XLA Ops:
  0.6 35.6 %copy-start = (f32[1024,128]{1,0:T(8,128)S(1)}, f32[1024,128]{1,0:T(8,128)}, u32[]{:S(2)}) copy-start(f32[1024,128]{1,0:T(8,128)} %param.18) | copy-start | bytes 1572868
  0.6 1.0 copy-start.3
  0.7 2.8 %copy-start.4 = (f32[256,64]{0,1:T(8,128)S(1)}, f32[256,64]{0,1:T(8,128)}, u32[]{:S(2)}) copy-start(f32[256,64]{0,1:T(8,128)} %param.17) | copy-start | bytes 196612
  36.9 24.4 %copy-start.1 = (f32[2,128,2,128]{3,2,1,0:T(2,128)S(1)}, f32[2,128,2,128]{3,2,1,0:T(2,128)}, u32[]{:S(2)}) copy-start(f32[2,128,2,128]{3,2,1,0:T(2,128)} %param.20) | copy-start | bytes 786436
  60.5 0.7 copy-start.8
  61.2 0.7 copy-start.7
  61.2 0.7 copy-start.6
  62.3 0.7 copy-start.9
  64.2 0.7 copy-start.5
  81.7 0.8 copy-start.2
  85.9 9.7 %all-to-all-start = ((f32[8,1,128]{2,1,0:T(1,128)}), f32[8,1,128]{2,1,0:T(1,128)S(1)}, u32[]{:S(2)}, u32[]{:S(2)}) async-start(f32[8,1,128]{2,1,0:T(1,128)} %bitcast.32), calls=%async_computation | async-start | bytes 8192 | tf_op jit(solution)/shard_map/all_to_all | solution.py:25
  89.2 0.7 copy-start.10
  95.6 25.7 %all-to-all-start.2 = ((f32[8,1,128]{2,1,0:T(1,128)}), f32[8,1,128]{2,1,0:T(1,128)S(1)}, u32[]{:S(2)}, u32[]{:S(2)}) async-start(f32[8,1,128]{2,1,0:T(1,128)} %bitcast.54), calls=%async_computation.2 | async-start | bytes 8192 | tf_op jit(solution)/shard_map/all_to_all | solution.py:25
  144.6 9.7 %all-to-all-start.3 = ((f32[8,1,128]{2,1,0:T(1,128)}), f32[8,1,128]{2,1,0:T(1,128)S(1)}, u32[]{:S(2)}, u32[]{:S(2)}) async-start(f32[8,1,128]{2,1,0:T(1,128)} %bitcast.75), calls=%async_computation.3 | async-start | bytes 8192 | tf_op jit(solution)/shard_map/all_to_all | solution.py:25
  178.2 9.7 %all-to-all-start.1 = ((f32[8,1,128]{2,1,0:T(1,128)}), f32[8,1,128]{2,1,0:T(1,128)S(1)}, u32[]{:S(2)}, u32[]{:S(2)}) async-start(f32[8,1,128]{2,1,0:T(1,128)} %bitcast.52), calls=%async_computation.1 | async-start | bytes 8192 | tf_op jit(solution)/shard_map/all_to_all | solution.py:25
where the time goes:
time: 189 us; the launch traced here: 188 us
  blocking collectives  135 us (71%)
  waiting for transfers between devices  17 us (9%)
  starting transfers between devices  13.2 us (7%)
  matrix products  8.39 us (4%)
  other arithmetic  7.59 us (4%)
  local copies, waits for them, and re-layouts  6.07 us (3%)
    all_gather x2, blocking collectives, tri_forward(): bias_full = lax.all_gather(bias_local, ('row', 'head'), axis=1, tiled=True)  37.2 us
    unnamed x2, blocking collectives  35.3 us
    all_gather x1, blocking collectives, body(): lax.all_gather(right_part, ('row', 'head'), axis=2, tiled=True)  32.3 us
    all_gather x1, blocking collectives, body(): lax.all_gather(mask_all, ('row', 'head'), axis=1, tiled=True)  20.4 us
    all_to_all x4, waiting for transfers between devices, reorient(): lax.all_to_all(turned, ('row', 'head'), split_axis=0, concat_axis=1, tile...  17 us
    all_to_all x4, starting transfers between devices, reorient(): lax.all_to_all(turned, ('row', 'head'), split_axis=0, concat_axis=1, tile...  13.2 us
    psum x4, blocking collectives, core_total(): return lax.psum(values, 'br')  9.82 us
    unnamed x26, local copies, waits for them, and re-layouts  4.8 us
  transfers between devices with their start and end apart: 4, of which 3 were waited for; matrix products, arithmetic and copies ran while one was open for 2% of the time, Pallas kernels for 0%

commit v1 on v0

--- a/solution.py
+++ b/solution.py
@@ -22,7 +22,15 @@
 
 def reorient(values):
     turned = jnp.swapaxes(values, 0, 1)
-    return lax.all_to_all(turned, ("row", "head"), split_axis=0, concat_axis=1, tiled=True)
+    return jnp.concatenate(
+        lax.all_to_all(
+            jnp.stack(jnp.split(turned, lax.axis_size(("row", "head")), axis=0)),
+            ("row", "head"),
+            0,
+            0,
+        ),
+        axis=1,
+    )
 
 
 def prepare(values, scales, weight_in, weight_bias):

time: 189 us -> 202 us (1.069)
  local copies, waits for them, and re-layouts: 6.07 us -> 22.6 us
  waiting for transfers between devices: 17 us -> 12.8 us
    unnamed x26 -> x56, local copies, waits for them, and re-layouts: 4.8 us -> 19.3 us
    all_to_all x4, waiting for transfers between devices: 17 us -> 12.8 us  [reorient(): lax.all_to_all(jnp.stack(jnp.split(turned, lax.axis_size(('row', 'head'))...]
    another operation x0 -> x4, local copies, waits for them, and re-layouts: none -> 2.05 us  [reorient(): jnp.stack(jnp.split(turned, lax.axis_size(('row', 'head')), axis=0))]
  transfers between devices with their start and end apart: 4 -> 4, of which waited for: 3 -> 3; matrix products, arithmetic and copies ran while one was open for 2% -> 4% of each run, Pallas kernels for 0% -> 0%
where the time goes in v1:
time: 202 us; the launch traced here: 201 us
  blocking collectives  135 us (67%)
  local copies, waits for them, and re-layouts  22.6 us (11%)
  starting transfers between devices  15.1 us (7%)
  waiting for transfers between devices  12.8 us (6%)
  matrix products  8.47 us (4%)
  other arithmetic  5.81 us (3%)
    all_gather x2, blocking collectives, tri_forward(): bias_full = lax.all_gather(bias_local, ('row', 'head'), axis=1, tiled=True)  37.3 us
    unnamed x2, blocking collectives  35.4 us
    all_gather x1, blocking collectives, body(): lax.all_gather(right_part, ('row', 'head'), axis=2, tiled=True)  32.3 us
    all_gather x1, blocking collectives, body(): lax.all_gather(mask_all, ('row', 'head'), axis=1, tiled=True)  20.4 us
    unnamed x56, local copies, waits for them, and re-layouts  19.3 us
    all_to_all x4, starting transfers between devices, reorient(): lax.all_to_all(jnp.stack(jnp.split(turned, lax.axis_size(('row', 'head'))...  15.1 us
    all_to_all x4, waiting for transfers between devices, reorient(): lax.all_to_all(jnp.stack(jnp.split(turned, lax.axis_size(('row', 'head'))...  12.8 us
    psum x4, blocking collectives, core_total(): return lax.psum(values, 'br')  9.82 us
  transfers between devices with their start and end apart: 4, of which 3 were waited for; matrix products, arithmetic and copies ran while one was open for 4% of the time, Pallas kernels for 0%

profile of v1, /device:TPU:0, one launch (start us, length us, event | category | flops | bytes accessed | tf_op | source)
XLA Modules:
  0.0 201.0 jit_solution(3927928212251576341)
XLA Ops:
  0.7 1.0 reduce_sum.121
  2.0 0.7 convert_bitcast_fusion
  2.6 0.8 multiply_multiply_fusion
  3.7 32.3 %all_gather.12 = f32[16,32,8]{1,0,2:T(8,128)S(1)} all-gather(f32[16,32,1]{1,0,2:T(8,128)S(1)} %fusion.30), channel_id=1, replica_groups=mesh['grp'=2,'row'=4,'head'=2,'br'=2] {'row','head'}, dimensions={2}, use_global_device_ids=true | all-gather | bytes 18432 | tf_op jit(solution)/shard_map/all_gather | solution.py:112
  36.9 0.7 convolution_bitcast_fusion.17
  37.6 2.5 %psum.35 = f32[1,8,128]{2,1,0:T(8,128)S(1)} all-reduce(f32[1,8,128]{2,1,0:T(8,128)S(1)} %convolution_bitcast_fusion.17), channel_id=1, replica_groups=mesh['grp'=2,'row'=4,'head'=2,'br'=2] {'br'}, use_global_device_ids=true, to_apply=%region_2.0 | all-reduce | flops 1024 | bytes 8192 | tf_op jit(solution)/shard_map/psum | solution.py:20
  40.0 20.4 %all-gather.2 = f32[8,1,32]{2,1,0:T(1,128)S(1)} all-gather(f32[1,1,32]{2,1,0:T(1,128)S(1)} %get-tuple-element.16), channel_id=1, replica_groups=mesh['grp'=2,'row'=4,'head'=2,'br'=2] {'row','head'}, dimensions={0}, use_global_device_ids=true | all-gather | bytes 1152 | tf_op jit(solution)/shard_map/all_gather | solution.py:113
  65.1 16.3 %all-gather.3 = f32[8,8,2]{1,2,0:T(2,128)S(1)} all-gather(f32[1,8,2]{1,2,0:T(2,128)S(1)} %convolution_bitcast_fusion.19), channel_id=2, replica_groups=mesh['grp'=2,'row'=4,'head'=2,'br'=2] {'row','head'}, dimensions={0}, use_global_device_ids=true | all-gather | bytes 576 | tf_op jit(solution)/shard_map/all_gather | solution.py:65
  82.8 2.5 %psum.36 = f32[1,8,128]{2,1,0:T(8,128)S(1)} all-reduce(f32[1,8,128]{2,1,0:T(8,128)S(1)} %convolution_bitcast_fusion.16), channel_id=1, replica_groups=mesh['grp'=2,'row'=4,'head'=2,'br'=2] {'br'}, use_global_device_ids=true, to_apply=%region_7.0 | all-reduce | flops 1024 | bytes 8192 | tf_op jit(solution)/shard_map/psum | solution.py:20
  89.4 3.4 %all-to-all-start = ((f32[8,1,1,128]{3,2,1,0:T(1,128)}), f32[8,1,1,128]{3,2,1,0:T(1,128)S(1)}, u32[]{:S(2)}, u32[]{:S(2)}) async-start(f32[8,1,1,128]{3,2,1,0:T(1,128)} %constant_dynamic-update-slice_fusion), calls=%async_computation | async-start | bytes 8192 | tf_op jit(solution)/shard_map/all_to_all | solution.py:26
  97.7 0.7 dynamic-slice
  98.3 0.9 all-to-all-done
  99.3 5.0 %all-to-all-start.2 = ((f32[8,1,1,128]{3,2,1,0:T(1,128)}), f32[8,1,1,128]{3,2,1,0:T(1,128)S(1)}, u32[]{:S(2)}, u32[]{:S(2)}) async-start(f32[8,1,1,128]{3,2,1,0:T(1,128)} %constant_dynamic-update-slice_fusion.16), calls=%async_computation.2 | async-start | bytes 8192 | tf_op jit(solution)/shard_map/all_to_all | solution.py:26
  104.8 21.0 %all-gather.4 = f32[8,8,2]{1,2,0:T(2,128)S(1)} all-gather(f32[1,8,2]{1,2,0:T(2,128)S(1)} %convolution_bitcast_fusion.18), channel_id=3, replica_groups=mesh['grp'=2,'row'=4,'head'=2,'br'=2] {'row','head'}, dimensions={0}, use_global_device_ids=true | all-gather | bytes 576 | tf_op jit(solution)/shard_map/all_gather | solution.py:65
  128.1 17.4 %all-reduce.8 = f32[2,8,8]{2,0,1:T(2,128)S(1)} all-reduce(f32[2,8,8]{2,0,1:T(2,128)S(1)} %copy.95), channel_id=4, replica_groups=mesh['grp'=2,'row'=4,'head'=2,'br'=2] {'row','head'}, use_global_device_ids=true, to_apply=%region_14.0.clone | all-reduce | flops 128 | bytes 1024
  145.5 0.9 fusion.90
  147.1 2.5 %psum.38 = f32[1,8,128]{2,1,0:T(8,128)S(1)} all-reduce(f32[1,8,128]{2,1,0:T(8,128)S(1)} %add_bitcast_fusion), channel_id=1, replica_groups=mesh['grp'=2,'row'=4,'head'=2,'br'=2] {'br'}, use_global_device_ids=true, to_apply=%region_17.0 | all-reduce | flops 1024 | bytes 8192 | tf_op jit(solution)/shard_map/psum | solution.py:20
  153.6 3.3 %all-to-all-start.3 = ((f32[8,1,1,128]{3,2,1,0:T(1,128)}), f32[8,1,1,128]{3,2,1,0:T(1,128)S(1)}, u32[]{:S(2)}, u32[]{:S(2)}) async-start(f32[8,1,1,128]{3,2,1,0:T(1,128)} %constant_dynamic-update-slice_fusion.24), calls=%async_computation.3 | async-start | bytes 8192 | tf_op jit(solution)/shard_map/all_to_all | solution.py:26
  157.2 6.1 %all-to-all-done.3 = f32[8,1,1,128]{3,2,1,0:T(1,128)S(1)} async-done(((f32[8,1,1,128]{3,2,1,0:T(1,128)}), f32[8,1,1,128]{3,2,1,0:T(1,128)S(1)}, u32[]{:S(2)}, u32[]{:S(2)}) %all-to-all-start.3) | async-done | bytes 4128 | tf_op jit(solution)/shard_map/all_to_all | solution.py:26
  164.6 17.9 %all-reduce.9 = f32[2,8,8]{2,0,1:T(2,128)S(1)} all-reduce(f32[2,8,8]{2,0,1:T(2,128)S(1)} %copy.97), channel_id=5, replica_groups=mesh['grp'=2,'row'=4,'head'=2,'br'=2] {'row','head'}, use_global_device_ids=true, to_apply=%region_19.0.clone | all-reduce | flops 128 | bytes 1024
  182.5 0.9 fusion.89
  184.1 2.5 %all-reduce.10 = (f32[1,8,128]{2,1,0:T(8,128)S(1)}, f32[1,8,128]{2,1,0:T(8,128)S(1)}) all-reduce(f32[1,8,128]{2,1,0:T(8,128)S(1)} %convolution_bitcast_fusion.15, f32[1,8,128]{2,1,0:T(8,128)S(1)} %broadcast_add_fusion), channel_id=1, replica_groups=mesh['grp'=2,'row'=4,'head'=2,'br'=2] {'br'}, use_global_device_ids=true, to_apply=%region_12.0 | all-reduce | flops 2048 | bytes 16384 | tf_op jit(solution)/shard_map/psum | solution.py:20
  190.7 3.3 %all-to-all-start.1 = ((f32[8,1,1,128]{3,2,1,0:T(1,128)}), f32[8,1,1,128]{3,2,1,0:T(1,128)S(1)}, u32[]{:S(2)}, u32[]{:S(2)}) async-start(f32[8,1,1,128]{3,2,1,0:T(1,128)} %constant_dynamic-update-slice_fusion.8), calls=%async_computation.1 | async-start | bytes 8192 | tf_op jit(solution)/shard_map/all_to_all | solution.py:26
  194.6 5.8 %all-to-all-done.1 = f32[8,1,1,128]{3,2,1,0:T(1,128)S(1)} async-done(((f32[8,1,1,128]{3,2,1,0:T(1,128)}), f32[8,1,1,128]{3,2,1,0:T(1,128)S(1)}, u32[]{:S(2)}, u32[]{:S(2)}) %all-to-all-start.1) | async-done | bytes 4128 | tf_op jit(solution)/shard_map/all_to_all | solution.py:26
  (135 shorter events, 31.3 us)
Async XLA Ops:
  0.6 35.6 %copy-start = (f32[1024,128]{1,0:T(8,128)S(1)}, f32[1024,128]{1,0:T(8,128)}, u32[]{:S(2)}) copy-start(f32[1024,128]{1,0:T(8,128)} %param.18) | copy-start | bytes 1572868
  0.6 1.0 copy-start.3
  0.7 2.8 %copy-start.4 = (f32[256,64]{0,1:T(8,128)S(1)}, f32[256,64]{0,1:T(8,128)}, u32[]{:S(2)}) copy-start(f32[256,64]{0,1:T(8,128)} %param.17) | copy-start | bytes 196612
  36.9 24.4 %copy-start.1 = (f32[2,128,2,128]{3,2,1,0:T(2,128)S(1)}, f32[2,128,2,128]{3,2,1,0:T(2,128)}, u32[]{:S(2)}) copy-start(f32[2,128,2,128]{3,2,1,0:T(2,128)} %param.20) | copy-start | bytes 786436
  60.5 0.7 copy-start.8
  61.2 0.7 copy-start.7
  61.2 0.7 copy-start.6
  62.3 0.7 copy-start.9
  64.2 0.7 copy-start.5
  81.7 0.8 copy-start.2
  89.4 3.5 %copy-start.10 = (f32[1,8,128]{2,1,0:T(8,128)S(1)}, f32[1,8,128]{2,1,0:T(8,128)}, u32[]{:S(2)}) copy-start(f32[1,8,128]{2,1,0:T(8,128)} %param.23) | copy-start | bytes 12292
  89.4 9.8 %all-to-all-start = ((f32[8,1,1,128]{3,2,1,0:T(1,128)}), f32[8,1,1,128]{3,2,1,0:T(1,128)S(1)}, u32[]{:S(2)}, u32[]{:S(2)}) async-start(f32[8,1,1,128]{3,2,1,0:T(1,128)} %constant_dynamic-update-slice_fusion), calls=%async_computation | async-start | bytes 8192 | tf_op jit(solution)/shard_map/all_to_all | solution.py:26
  97.0 0.7 copy-start.11
  99.3 27.5 %all-to-all-start.2 = ((f32[8,1,1,128]{3,2,1,0:T(1,128)}), f32[8,1,1,128]{3,2,1,0:T(1,128)S(1)}, u32[]{:S(2)}, u32[]{:S(2)}) async-start(f32[8,1,1,128]{3,2,1,0:T(1,128)} %constant_dynamic-update-slice_fusion.16), calls=%async_computation.2 | async-start | bytes 8192 | tf_op jit(solution)/shard_map/all_to_all | solution.py:26
  153.6 9.7 %all-to-all-start.3 = ((f32[8,1,1,128]{3,2,1,0:T(1,128)}), f32[8,1,1,128]{3,2,1,0:T(1,128)S(1)}, u32[]{:S(2)}, u32[]{:S(2)}) async-start(f32[8,1,1,128]{3,2,1,0:T(1,128)} %constant_dynamic-update-slice_fusion.24), calls=%async_computation.3 | async-start | bytes 8192 | tf_op jit(solution)/shard_map/all_to_all | solution.py:26
  190.7 9.7 %all-to-all-start.1 = ((f32[8,1,1,128]{3,2,1,0:T(1,128)}), f32[8,1,1,128]{3,2,1,0:T(1,128)S(1)}, u32[]{:S(2)}, u32[]{:S(2)}) async-start(f32[8,1,1,128]{3,2,1,0:T(1,128)} %constant_dynamic-update-slice_fusion.8), calls=%async_computation.1 | async-start | bytes 8192 | tf_op jit(solution)/shard_map/all_to_all | solution.py:26
